TPU v7x, 32 devices: a whole 2x2x4 slice. The times are simulated.
32 devices in a mesh: seq: 8 (over z, core), head: 4 (over y, x).
Axes of the slice: x: 2, y: 2, z: 4, core: 2. Of those that a mesh axis runs over, the one named last changes fastest.
Arguments:
- tokens: bfloat16 [1024, 4096], P('seq', 'head'), may hold values from -6 to 6
- w_query: bfloat16 [4096, 4096], P(None, 'head'), may hold values from -0.09375 to 0.09375
- w_key: bfloat16 [4096, 4096], P(None, 'head'), may hold values from -0.09375 to 0.09375
- w_value: bfloat16 [4096, 4096], P(None, 'head'), may hold values from -0.09375 to 0.09375
- upstream: bfloat16 [1024, 4096], P('seq', 'head'), may hold values from -6 to 6
- log_decay: float32 [1024, 32], P('seq', 'head'), may hold values from -1 to 0, as said below
- segment: int32 [1024], replicated, may hold values from 0 to 7, never falling along the last dimension, each value on 1 to 256 neighbouring positions
Outputs:
- grad_query: bfloat16 [4096, 4096], P('seq', 'head')
- grad_key: bfloat16 [4096, 4096], P('seq', 'head')
- grad_value: bfloat16 [4096, 4096], P('seq', 'head')
Inputs may be any that keep to these rules, and one draw needn't show every extreme that they name: log_decay is negative. `segment`: document ids never fall along the tokens; each document holds 1 to 256 tokens.
All inputs are finite; a program needn't handle non-finite values.
Results may differ from a plain program's by a relative error of at most 0.02.
Values may be sent and summed in bfloat16 or wider, within the bound.
No kernel may reach another device: no remote copies, remote signals or barrier semaphores. Data moves between devices by JAX's collectives and lax.ppermute only.
A program may use at most 64 MiB of HBM per device.

v0:
```python
import jax
import jax.numpy as jnp
from jax import lax
from jax.sharding import PartitionSpec as P

HEAD = 128


def carried_in(x, axis, combine, identity, reverse):
    count, place = (lax.axis_size(axis), lax.axis_index(axis))
    everything = jax.tree.map(
        lambda part, kind: lax.all_gather(part.astype(kind), axis), x, (jnp.bfloat16, jnp.bfloat16)
    )
    start = jax.tree.map(
        lambda part, zero: jnp.broadcast_to(jnp.asarray(zero, part.dtype), part.shape), x, identity
    )

    def turn(k, before):
        at = count - 1 - k if reverse else k
        reached = at > place if reverse else at < place
        new = combine(
            before, jax.tree.map(lambda part, own: part[at].astype(own.dtype), everything, x)
        )
        return jax.tree.map(lambda a, b: jnp.where(reached, a, b), new, before)

    return lax.fori_loop(0, count, turn, start)


def block_factors(log_rates, segs, previous):
    log_sum = jnp.cumsum(log_rates, axis=0)
    last_sum = log_sum[-1]
    last_seg = segs[-1]
    state_entering = jnp.where((segs == previous)[:, None], jnp.exp(log_sum), 0.0)
    state_leaving = jnp.where(
        (segs == last_seg)[:, None], jnp.exp(last_sum[None, :] - log_sum), 0.0
    )
    carry_decay = jnp.where(last_seg == previous, jnp.exp(last_sum), 0.0)
    places = jnp.arange(segs.shape[0], dtype=jnp.int32)
    same = (segs[:, None] == segs[None, :]) & (places[:, None] >= places[None, :])
    spread = log_sum.T[:, :, None] - log_sum.T[:, None, :]
    decay_mat = jnp.where(
        same[None], HEAD ** (-0.5) * jnp.exp(jnp.where(same[None], spread, 0.0)), 0.0
    )
    return (state_entering, state_leaving, carry_decay, decay_mat)


def combine(earlier, later):
    return (earlier[0] * later[0], later[0][:, None, None] * earlier[1] + later[1])


def local(tokens, w_query, w_key, w_value, upstream, log_decay, segment):
    rows = tokens.shape[0]
    width = w_query.shape[1]
    heads = width // HEAD
    piece = lax.all_gather(tokens, "head", axis=1, tiled=True)

    def partial_product(weight):
        return jnp.dot(piece, weight, preferred_element_type=jnp.float32)

    query_sum = partial_product(w_query)
    key_sum = partial_product(w_key)
    value_sum = partial_product(w_value)
    query = query_sum.astype(jnp.bfloat16).reshape(rows, heads, HEAD)
    key_rows = key_sum.astype(jnp.bfloat16).reshape(rows, heads, HEAD)
    value_rows = value_sum.astype(jnp.bfloat16).reshape(rows, heads, HEAD)
    output_gradient = upstream.reshape(rows, heads, HEAD)
    my_index = lax.axis_index("seq")
    first = my_index * rows
    segs = lax.dynamic_slice_in_dim(segment, first, rows)
    before = lax.dynamic_slice_in_dim(segment, jnp.maximum(first - 1, 0), 1)[0]
    previous = jnp.where(my_index > 0, before, jnp.int32(-1))
    state_entering, state_leaving, carry_decay, decay_mat = block_factors(log_decay, segs, previous)
    scale = HEAD ** (-0.5)
    weighted_keys = (scale * state_leaving[:, :, None] * key_rows).astype(jnp.bfloat16)
    segment_state = jnp.einsum(
        "bdw,bdq->dwq", weighted_keys, value_rows, preferred_element_type=jnp.float32
    )
    weighted_queries = (scale * state_entering[:, :, None] * query).astype(jnp.bfloat16)
    following_state = jnp.einsum(
        "bdw,bdq->dwq", weighted_queries, output_gradient, preferred_element_type=jnp.float32
    )
    identity = (jnp.ones_like(carry_decay), jnp.zeros_like(segment_state))
    arriving_state = carried_in((carry_decay, segment_state), "seq", combine, identity, False)[1]
    backward_state = carried_in((carry_decay, following_state), "seq", combine, identity, True)[1]
    upper_limit = lax.Precision.HIGHEST
    score_qk = jnp.einsum("thd,shd->hts", query, key_rows, preferred_element_type=jnp.float32)
    attention_query_key = (decay_mat * score_qk).astype(jnp.bfloat16)
    score_up = jnp.einsum(
        "thd,shd->hts", output_gradient, value_rows, preferred_element_type=jnp.float32
    )
    attention_upstream = (decay_mat * score_up).astype(jnp.bfloat16)
    output_gradient_float = output_gradient.astype(jnp.float32)
    query_gradient = jnp.einsum(
        "wcz,zwm->cwm", attention_upstream, key_rows, preferred_element_type=jnp.float32
    ) + state_entering[:, :, None] * jnp.einsum(
        "pzo,zao->pza", output_gradient_float, arriving_state, precision=upper_limit
    )
    key_gradient = jnp.einsum(
        "voi,ovw->ivw", attention_upstream, query, preferred_element_type=jnp.float32
    ) + state_leaving[:, :, None] * jnp.einsum(
        "ixz,xqz->ixq", value_rows.astype(jnp.float32), backward_state, precision=upper_limit
    )
    value_gradient = jnp.einsum(
        "voi,ovw->ivw", attention_query_key, output_gradient, preferred_element_type=jnp.float32
    ) + state_leaving[:, :, None] * jnp.einsum(
        "dqg,qgf->dqf", key_rows.astype(jnp.float32), backward_state, precision=upper_limit
    )
    grads = jnp.concatenate(
        [
            query_gradient.astype(jnp.bfloat16).reshape(rows, width),
            key_gradient.astype(jnp.bfloat16).reshape(rows, width),
            value_gradient.astype(jnp.bfloat16).reshape(rows, width),
        ],
        axis=1,
    )
    contract = (((0,), (0,)), ((), ()))
    columns = lax.all_to_all(piece, "seq", split_axis=1, concat_axis=0, tiled=True)
    every = lax.all_gather(grads, "seq", axis=0, tiled=True)
    sums = lax.dot_general(columns, every, contract, preferred_element_type=jnp.float32)
    grad_query = sums[:, :width].astype(jnp.bfloat16)
    grad_key = sums[:, width : 2 * width].astype(jnp.bfloat16)
    grad_value = sums[:, 2 * width :].astype(jnp.bfloat16)
    return (grad_query, grad_key, grad_value)


def solution(mesh):
    placed = (
        P("seq", "head"),
        P(None, "head"),
        P(None, "head"),
        P(None, "head"),
        P("seq", "head"),
        P("seq", "head"),
        P(),
    )
    return jax.shard_map(
        local,
        mesh=mesh,
        in_specs=placed,
        out_specs=(P("seq", "head"), P("seq", "head"), P("seq", "head")),
        check_vma=False,
    )
```

profile of v0, /device:TPU:0, one launch (start us, length us, event | category | flops | bytes accessed | tf_op | source)
XLA Modules:
  0.0 217.6 jit_solution(17565093690592653566)
XLA Ops:
  7.2 1.8 copy.124
  9.1 1.3 dynamic_slice.41
  14.0 1.1 copy.160
  15.9 23.7 %all-gather.8.cloned.1.call-done = bf16[128,4096]{0,1:T(8,128)(2,1)} async-done(((bf16[128,1024]{0,1:T(8,128)(2,1)}), bf16[128,4096]{0,1:T(8,128)(2,1)}) %all-gather.8.cloned.1.call-update) | async-done | bytes 1048592 | tf_op jit(solution)/shard_map/all_gather | solution.py:55
  39.6 5.1 %convolution_convert_fusion.2 = bf16[128,1024]{1,0:T(8,128)(2,1)S(1)} fusion(bf16[128,4096]{0,1:T(8,128)(2,1)} %all-gather.8.cloned.1.call-done, bf16[4096,1024]{1,0:T(8,128)(2,1)} %param.12), kind=kOutput, calls=%fused_computation.24 | convolution fusion | flops 1073872896 | bytes 9699328 | tf_op jit(solution)/shard_map/dot_general | solution.py:58
  46.0 11.7 %all-gather.2 = bf16[8,1,8]{2,1,0:T(2,128)(2,1)S(1)} all-gather(bf16[1,1,8]{2,1,0:T(2,128)(2,1)S(1)} %get-tuple-element.312), channel_id=1, replica_groups=mesh['seq'=8,'head'=4] {'seq'}, dimensions={0}, use_global_device_ids=true | all-gather | bytes 144 | tf_op jit(solution)/shard_map/all_gather | solution.py:12
  57.9 4.7 %convolution_convert_fusion.5 = bf16[128,1024]{1,0:T(8,128)(2,1)S(1)} fusion(bf16[128,4096]{0,1:T(8,128)(2,1)S(1)} %copy-done, bf16[4096,1024]{1,0:T(8,128)(2,1)} %param.13), kind=kOutput, calls=%fused_computation.27 | convolution fusion | flops 1073872896 | bytes 9699328 | tf_op jit(solution)/shard_map/dot_general | solution.py:58
  62.8 4.7 %fusion.15 = bf16[16,8,8,128]{3,2,1,0:T(8,128)(2,1)S(1)} fusion(bf16[128,4096]{0,1:T(8,128)(2,1)S(1)} %copy-done, bf16[4096,1024]{1,0:T(8,128)(2,1)} %param.14), kind=kOutput, calls=%fused_computation.33 | convolution fusion | flops 1073872896 | bytes 9699328 | tf_op jit(solution)/shard_map/dot_general | solution.py:58
  68.8 6.5 %all-gather.14.cloned.1.call-done = bf16[64,128,128]{2,1,0:T(8,128)(2,1)} async-done(((bf16[8,128,128]{2,1,0:T(8,128)(2,1)}), bf16[64,128,128]{2,1,0:T(8,128)(2,1)}) %all-gather.14.cloned.1.call-update) | async-done | bytes 2097168 | tf_op jit(solution)/shard_map/all_gather | solution.py:12
  75.2 9.1 %while.31 = (s32[]{:T(128)}, f32[8,128,128]{2,1,0:T(8,128)S(1)}, s32[]{:T(128)}, bf16[8,8]{1,0:T(8,128)(2,1)S(1)}, bf16[8,8,128,128]{3,2,1,0:T(8,128)(2,1)}, /*index=5*/s32[]{:T(128)}, s32[]{:T(128)}, s32[]{:T(128)}, s32[]{:T(128)}) while((s32[]{:T(128)}, f32[8,128,128]{2,1,0:T(8,128)S(1)}, s32[]{:T(128)}, ...), condition=%wide.region_4.5_spmd.clone, body=%wide.region_3.4_spmd.clone.sunk | while | flops 655376 | bytes 1310975 | solution.py:26
  82.1 1.1 fusion.60
  83.2 1.1 fusion.60
  84.3 1.5 fusion.8
  85.8 1.4 fusion.9
  87.2 2.3 %fusion.11 = bf16[128,8,128]{0,2,1:T(8,128)(2,1)} fusion(f32[128,8,128]{0,2,1:T(8,128)} %fusion.9, bf16[128,8,128]{0,2,1:T(8,128)(2,1)S(1)} %bitcast.118, bf16[128,8,128]{0,2,1:T(8,128)(2,1)S(1)} %bitcast.121, bf16[128,8,128]{0,2,1:T(8,128)(2,1)S(1)} %bitcast.113, f32[8,128]{1,0:T(8,128)S(1)} %copy.126, pred[128,128]{0,1:T(8,128)(4,1)S(1)} %fusion.29), kind=kOutput, calls=%fused_computation.29 | convolution fusion | flops 68157440 | bytes 1593344 | tf_op jit(solution)/shard_map/voi,ovw->ivw/dot_general | solution.py:103
  89.5 15.9 %all-gather.12.cloned.1.call-done = bf16[64,128,128]{2,1,0:T(8,128)(2,1)} async-done(((bf16[8,128,128]{2,1,0:T(8,128)(2,1)}), bf16[64,128,128]{2,1,0:T(8,128)(2,1)}) %all-gather.12.cloned.1.call-update) | async-done | bytes 2097168 | tf_op jit(solution)/shard_map/all_gather | solution.py:12
  105.4 9.0 %while.30 = (s32[]{:T(128)}, f32[8,128,128]{2,1,0:T(8,128)S(1)}, s32[]{:T(128)}, bf16[8,8]{1,0:T(8,128)(2,1)S(1)}, bf16[8,8,128,128]{3,2,1,0:T(8,128)(2,1)}, /*index=5*/s32[]{:T(128)}, s32[]{:T(128)}) while((s32[]{:T(128)}, f32[8,128,128]{2,1,0:T(8,128)S(1)}, s32[]{:T(128)}, bf16[8,8]{1,0:T(8,128)(2,1)S(1)}, ...), condition=%wide.region_2.3_spmd.clone, body=%wide.region_1.2_spmd.clone.sunk | while | flops 655372 | bytes 1310913 | solution.py:26
  115.4 1.9 pad_maximum_fusion
  117.3 55.8 %all_to_all.19 = bf16[128,8,512]{0,2,1:T(8,128)(2,1)S(1)} all-to-all(bf16[128,8,512]{0,2,1:T(8,128)(2,1)S(1)} %bitcast.110), channel_id=1, replica_groups=mesh['seq'=8,'head'=4] {'seq'}, dimensions={1} | all-to-all | bytes 2097152 | tf_op jit(solution)/shard_map/all_to_all | solution.py:117
  173.6 26.8 %all-gather.10.cloned.1.call-done = bf16[1024,3072]{0,1:T(8,128)(2,1)} async-done(((bf16[128,3072]{0,1:T(8,128)(2,1)}), bf16[1024,3072]{0,1:T(8,128)(2,1)}) %all-gather.10.cloned.1.call-update) | async-done | bytes 6291472 | tf_op jit(solution)/shard_map/all_gather | solution.py:118
  200.4 6.4 %fusion.2 = bf16[512,3072]{0,1:T(8,128)(2,1)S(1)} fusion(bf16[1024,3072]{0,1:T(8,128)(2,1)} %all-gather.10.cloned.1.call-done, bf16[1024,512]{1,0:T(8,128)(2,1)S(1)} %bitcast.123), kind=kOutput, calls=%fused_computation.7 | convolution fusion | flops 3222798336 | bytes 10485760 | tf_op jit(solution)/shard_map/dot_general | solution.py:119
  207.1 1.3 copy.152
  208.4 1.3 copy.151
  209.7 1.3 copy.150
  (65 shorter events, 23.1 us)
Async XLA Ops:
  7.2 32.5 %all-gather.8.cloned.1.call-start = ((), (), s32[]{:S(2)}) async-start(), calls=%async_computation.1 | async-start | bytes 1310720 | tf_op jit(solution)/shard_map/all_gather | solution.py:55
  9.0 66.2 %all-gather.14.cloned.1.call-start = ((), (), s32[]{:S(2)}) async-start(), calls=%async_computation.4 | async-start | bytes 2359296 | tf_op jit(solution)/shard_map/all_gather | solution.py:12
  39.6 18.2 %copy-start = (bf16[128,4096]{0,1:T(8,128)(2,1)S(1)}, bf16[128,4096]{0,1:T(8,128)(2,1)}, u32[]{:S(2)}) copy-start(bf16[128,4096]{0,1:T(8,128)(2,1)} %all-gather.8.cloned.1.call-done) | copy-start | bytes 3145732
  45.9 59.5 %all-gather.12.cloned.1.call-start = ((), (), s32[]{:S(2)}) async-start(), calls=%async_computation.3 | async-start | bytes 2359296 | tf_op jit(solution)/shard_map/all_gather | solution.py:12
  68.5 132.0 %all-gather.10.cloned.1.call-start = ((), (), s32[]{:S(2)}) async-start(), calls=%async_computation.2 | async-start | bytes 7077888 | tf_op jit(solution)/shard_map/all_gather | solution.py:118
  87.2 27.3 %copy-start.1 = (f32[128,8,128]{0,2,1:T(8,128)S(1)}, f32[128,8,128]{0,2,1:T(8,128)}, u32[]{:S(2)}) copy-start(f32[128,8,128]{0,2,1:T(8,128)} %fusion.8) | copy-start | bytes 1572868
Sparse Core Ops, SparseCore 0:
  10.4 29.2 all-gather.7
  46.0 29.1 all-gather.13
  76.8 28.5 all-gather.11
  117.4 82.9 all-gather.9
where the time goes:
time: 219 us; the launch traced here: 218 us
  waiting for transfers between devices  73 us (33%)
  blocking collectives  67.5 us (31%)
  matrix products  29.1 us (13%)
  other arithmetic  21.3 us (10%)
  between operations  15.3 us (7%)
  local copies, waits for them, and re-layouts  10.7 us (5%)
    all_to_all x1, blocking collectives, local(): lax.all_to_all(piece, 'seq', split_axis=1, concat_axis=0, tiled=True)  55.8 us
    all_gather x1, waiting for transfers between devices, local(): every = lax.all_gather(grads, 'seq', axis=0, tiled=True)  26.8 us
    all_gather x1, waiting for transfers between devices, local(): piece = lax.all_gather(tokens, 'head', axis=1, tiled=True)  23.7 us
    all_gather x2, waiting for transfers between devices, carried_in(): lax.all_gather(part.astype(kind), axis)  22.4 us
    select_n x16, other arithmetic, turn(): return jax.tree.map(lambda a, b: jnp.where(reached, a, b), new, before)  17.5 us
    dot_general x3, matrix products, partial_product(): return jnp.dot(piece, weight, preferred_element_type=jnp.float32)  14.5 us
    all_gather x1, blocking collectives, carried_in(): lax.all_gather(part.astype(kind), axis)  11.7 us
    unnamed x10, local copies, waits for them, and re-layouts  6.52 us
  transfers between devices with their start and end apart: 4, of which 4 were waited for; matrix products, arithmetic and copies ran while one was open for 14% of the time, Pallas kernels for 0%

commit v1 on v0

--- a/solution.py
+++ b/solution.py
@@ -2,6 +2,7 @@
 import jax.numpy as jnp
 from jax import lax
 from jax.sharding import PartitionSpec as P
+from jax.lax import all_to_all, psum
 
 HEAD = 128
 
@@ -114,7 +115,15 @@
         axis=1,
     )
     contract = (((0,), (0,)), ((), ()))
-    columns = lax.all_to_all(piece, "seq", split_axis=1, concat_axis=0, tiled=True)
+    columns = jnp.concatenate(
+        all_to_all(
+            jnp.stack(jnp.split(piece, psum(1, axis_name="seq"), axis=1), axis=0),
+            axis_name="seq",
+            split_axis=0,
+            concat_axis=0,
+        ),
+        0,
+    )
     every = lax.all_gather(grads, "seq", axis=0, tiled=True)
     sums = lax.dot_general(columns, every, contract, preferred_element_type=jnp.float32)
     grad_query = sums[:, :width].astype(jnp.bfloat16)

time: 219 us -> 216 us (0.986)
  local copies, waits for them, and re-layouts: 10.7 us -> 6.04 us
    unnamed x10 -> x13, local copies, waits for them, and re-layouts: 6.52 us -> 0.88 us
where the time goes in v1:
time: 216 us; the launch traced here: 215 us
  waiting for transfers between devices  74.8 us (35%)
  blocking collectives  67.5 us (31%)
  matrix products  29.3 us (14%)
  other arithmetic  21.3 us (10%)
  between operations  15.3 us (7%)
  local copies, waits for them, and re-layouts  6.04 us (3%)
    all_to_all x1, blocking collectives, local(): all_to_all(jnp.stack(jnp.split(piece, psum(1, axis_name='seq'), axis=1),...  55.8 us
    all_gather x1, waiting for transfers between devices, local(): every = lax.all_gather(grads, 'seq', axis=0, tiled=True)  27.3 us
    all_gather x1, waiting for transfers between devices, local(): piece = lax.all_gather(tokens, 'head', axis=1, tiled=True)  24.3 us
    all_gather x2, waiting for transfers between devices, carried_in(): lax.all_gather(part.astype(kind), axis)  22.4 us
    select_n x16, other arithmetic, turn(): return jax.tree.map(lambda a, b: jnp.where(reached, a, b), new, before)  17.5 us
    dot_general x3, matrix products, partial_product(): return jnp.dot(piece, weight, preferred_element_type=jnp.float32)  14.4 us
    all_gather x1, blocking collectives, carried_in(): lax.all_gather(part.astype(kind), axis)  11.7 us
    dot_general x1, matrix products, local(): lax.dot_general(columns, every, contract, preferred_element_type=jnp.floa...  6.6 us
  transfers between devices with their start and end apart: 4, of which 4 were waited for; matrix products, arithmetic and copies ran while one was open for 14% of the time, Pallas kernels for 0%

profile of v1, /device:TPU:0, one launch (start us, length us, event | category | flops | bytes accessed | tf_op | source)
XLA Modules:
  0.0 214.9 jit_solution(16309622872515801517)
XLA Ops:
  8.0 1.3 dynamic_slice.41
  12.9 1.1 copy.113
  14.8 24.3 %all-gather.8.cloned.1.call-done = bf16[128,4096]{1,0:T(8,128)(2,1)} async-done(((bf16[128,1024]{1,0:T(8,128)(2,1)}), bf16[128,4096]{1,0:T(8,128)(2,1)}) %all-gather.8.cloned.1.call-update) | async-done | bytes 1048592 | tf_op jit(solution)/shard_map/all_gather | solution.py:56
  39.1 5.0 %convolution_convert_fusion.2 = bf16[128,1024]{1,0:T(8,128)(2,1)S(1)} fusion(bf16[128,4096]{1,0:T(8,128)(2,1)} %all-gather.8.cloned.1.call-done, bf16[4096,1024]{1,0:T(8,128)(2,1)} %param.12), kind=kOutput, calls=%fused_computation.23 | convolution fusion | flops 1073872896 | bytes 9699328 | tf_op jit(solution)/shard_map/dot_general | solution.py:59
  45.4 11.7 %all-gather.2 = bf16[8,1,8]{2,1,0:T(2,128)(2,1)S(1)} all-gather(bf16[1,1,8]{2,1,0:T(2,128)(2,1)S(1)} %get-tuple-element.297), channel_id=1, replica_groups=mesh['seq'=8,'head'=4] {'seq'}, dimensions={0}, use_global_device_ids=true | all-gather | bytes 144 | tf_op jit(solution)/shard_map/all_gather | solution.py:13
  57.3 4.7 %convolution_convert_fusion.5 = bf16[128,1024]{1,0:T(8,128)(2,1)S(1)} fusion(bf16[128,4096]{1,0:T(8,128)(2,1)S(1)} %copy-done, bf16[4096,1024]{1,0:T(8,128)(2,1)} %param.13), kind=kOutput, calls=%fused_computation.26 | convolution fusion | flops 1073872896 | bytes 9699328 | tf_op jit(solution)/shard_map/dot_general | solution.py:59
  62.1 4.7 %fusion.14 = bf16[16,8,8,128]{3,2,1,0:T(8,128)(2,1)S(1)} fusion(bf16[128,4096]{1,0:T(8,128)(2,1)S(1)} %copy-done, bf16[4096,1024]{1,0:T(8,128)(2,1)} %param.14), kind=kOutput, calls=%fused_computation.32 | convolution fusion | flops 1073872896 | bytes 9699328 | tf_op jit(solution)/shard_map/dot_general | solution.py:59
  68.1 6.5 %all-gather.14.cloned.1.call-done = bf16[64,128,128]{2,1,0:T(8,128)(2,1)} async-done(((bf16[8,128,128]{2,1,0:T(8,128)(2,1)}), bf16[64,128,128]{2,1,0:T(8,128)(2,1)}) %all-gather.14.cloned.1.call-update) | async-done | bytes 2097168 | tf_op jit(solution)/shard_map/all_gather | solution.py:13
  74.6 9.1 %while.31 = (s32[]{:T(128)}, f32[8,128,128]{2,1,0:T(8,128)S(1)}, s32[]{:T(128)}, bf16[8,8]{1,0:T(8,128)(2,1)S(1)}, bf16[8,8,128,128]{3,2,1,0:T(8,128)(2,1)}, /*index=5*/s32[]{:T(128)}, s32[]{:T(128)}, s32[]{:T(128)}, s32[]{:T(128)}) while((s32[]{:T(128)}, f32[8,128,128]{2,1,0:T(8,128)S(1)}, s32[]{:T(128)}, ...), condition=%wide.region_4.5_spmd.clone, body=%wide.region_3.4_spmd.clone.sunk | while | flops 655376 | bytes 1310975 | solution.py:27
  75.8 1.1 fusion.67
  76.9 1.1 fusion.67
  78.1 1.1 fusion.67
  81.5 1.1 fusion.67
  82.6 1.1 fusion.67
  83.7 1.5 fusion.7
  85.2 1.4 fusion.8
  86.6 2.3 %fusion.10 = bf16[128,8,128]{0,2,1:T(8,128)(2,1)} fusion(f32[128,8,128]{0,2,1:T(8,128)} %fusion.8, bf16[128,8,128]{0,2,1:T(8,128)(2,1)S(1)} %bitcast.144, bf16[128,8,128]{0,2,1:T(8,128)(2,1)S(1)} %bitcast.147, bf16[128,8,128]{0,2,1:T(8,128)(2,1)S(1)} %bitcast.140, f32[8,128]{1,0:T(8,128)S(1)} %copy.83, pred[128,128]{0,1:T(8,128)(4,1)S(1)} %fusion.36), kind=kOutput, calls=%fused_computation.28 | convolution fusion | flops 68157440 | bytes 1593344 | tf_op jit(solution)/shard_map/voi,ovw->ivw/dot_general | solution.py:104
  88.9 15.9 %all-gather.12.cloned.1.call-done = bf16[64,128,128]{2,1,0:T(8,128)(2,1)} async-done(((bf16[8,128,128]{2,1,0:T(8,128)(2,1)}), bf16[64,128,128]{2,1,0:T(8,128)(2,1)}) %all-gather.12.cloned.1.call-update) | async-done | bytes 2097168 | tf_op jit(solution)/shard_map/all_gather | solution.py:13
  104.8 9.0 %while.30 = (s32[]{:T(128)}, f32[8,128,128]{2,1,0:T(8,128)S(1)}, s32[]{:T(128)}, bf16[8,8]{1,0:T(8,128)(2,1)S(1)}, bf16[8,8,128,128]{3,2,1,0:T(8,128)(2,1)}, /*index=5*/s32[]{:T(128)}, s32[]{:T(128)}) while((s32[]{:T(128)}, f32[8,128,128]{2,1,0:T(8,128)S(1)}, s32[]{:T(128)}, bf16[8,8]{1,0:T(8,128)(2,1)S(1)}, ...), condition=%wide.region_2.3_spmd.clone, body=%wide.region_1.2_spmd.clone.sunk | while | flops 655372 | bytes 1310913 | solution.py:27
  114.8 1.9 pad_maximum_fusion
  116.8 55.8 %all_to_all.5 = bf16[8,128,512]{2,1,0:T(8,128)(2,1)S(1)} all-to-all(bf16[8,128,512]{2,1,0:T(8,128)(2,1)S(1)} %fusion.28), channel_id=1, replica_groups=mesh['seq'=8,'head'=4] {'seq'}, dimensions={0} | all-to-all | bytes 2097152 | tf_op jit(solution)/shard_map/all_to_all | solution.py:119
  172.7 27.3 %all-gather.10.cloned.1.call-done = bf16[1024,3072]{0,1:T(8,128)(2,1)} async-done(((bf16[128,3072]{0,1:T(8,128)(2,1)}), bf16[1024,3072]{0,1:T(8,128)(2,1)}) %all-gather.10.cloned.1.call-update) | async-done | bytes 6291472 | tf_op jit(solution)/shard_map/all_gather | solution.py:127
  200.0 6.6 %convolution_convert_fusion = bf16[512,3072]{1,0:T(8,128)(2,1)S(1)} fusion(bf16[1024,512]{1,0:T(8,128)(2,1)S(1)} %bitcast.149, bf16[1024,3072]{0,1:T(8,128)(2,1)} %all-gather.10.cloned.1.call-done), kind=kOutput, calls=%fused_computation.6 | convolution fusion | flops 3222798336 | bytes 10485760 | tf_op jit(solution)/shard_map/dot_general | solution.py:128
  206.6 1.7 fusion.41
  (68 shorter events, 19.8 us)
Async XLA Ops:
  7.2 31.9 %all-gather.8.cloned.1.call-start = ((), (), s32[]{:S(2)}) async-start(), calls=%async_computation.1 | async-start | bytes 1310720 | tf_op jit(solution)/shard_map/all_gather | solution.py:56
  7.9 66.7 %all-gather.14.cloned.1.call-start = ((), (), s32[]{:S(2)}) async-start(), calls=%async_computation.4 | async-start | bytes 2359296 | tf_op jit(solution)/shard_map/all_gather | solution.py:13
  39.1 18.2 %copy-start = (bf16[128,4096]{1,0:T(8,128)(2,1)S(1)}, bf16[128,4096]{1,0:T(8,128)(2,1)}, u32[]{:S(2)}) copy-start(bf16[128,4096]{1,0:T(8,128)(2,1)} %all-gather.8.cloned.1.call-done) | copy-start | bytes 3145732
  45.3 59.5 %all-gather.12.cloned.1.call-start = ((), (), s32[]{:S(2)}) async-start(), calls=%async_computation.3 | async-start | bytes 2359296 | tf_op jit(solution)/shard_map/all_gather | solution.py:13
  67.8 132.2 %all-gather.10.cloned.1.call-start = ((), (), s32[]{:S(2)}) async-start(), calls=%async_computation.2 | async-start | bytes 7077888 | tf_op jit(solution)/shard_map/all_gather | solution.py:127
  86.6 27.3 %copy-start.1 = (f32[128,8,128]{0,2,1:T(8,128)S(1)}, f32[128,8,128]{0,2,1:T(8,128)}, u32[]{:S(2)}) copy-start(f32[128,8,128]{0,2,1:T(8,128)} %fusion.7) | copy-start | bytes 1572868
Sparse Core Ops, SparseCore 0:
  9.8 29.2 all-gather.7
  45.5 29.1 all-gather.13
  76.2 28.5 all-gather.11
  116.8 83.1 all-gather.9
